TPU v7x, 32 devices: a whole 2x2x4 slice. The times are simulated.
32 devices in a mesh: row: 8 (over y, x, core), col: 4 (over z).
Axes of the slice: x: 2, y: 2, z: 4, core: 2. Of those that a mesh axis runs over, the one named last changes fastest.
Arguments:
- matrix: float32 [16384, 8192], P('row', 'col'), may hold values from -40 to 40
Outputs:
- upper: float32 [256, 8192], P('row', 'col')
- reduced: float32 [16384, 8192], P('row', 'col')
All inputs are finite; a program needn't handle non-finite values.
Results may differ from a plain program's by a relative error of at most 0.0003.
Values sent between devices are 32-bit elements; how exact they have to be, the bound alone decides.
A program may use at most 128 MiB of HBM per device.

v0:
```python
import jax
import jax.numpy as jnp
from jax import lax
from jax.sharding import PartitionSpec as P

PANEL = 256


precise = lax.Precision.HIGHEST


def broadcast(shard, axis, root):
    mine = lax.axis_index(axis) == root
    return lax.psum(jnp.where(mine, shard, jnp.zeros_like(shard)), axis)


def multiply(left, right):
    return jnp.dot(left, right, precision=precise, preferred_element_type=jnp.float32)


def cholesky_pass(block):
    gram = multiply(block.T, block)
    lower = jnp.linalg.cholesky(gram)
    basis = jax.scipy.linalg.solve_triangular(lower, block.T, lower=True).T
    return (basis, lower.T)


def factorize(block):
    first_basis, first_upper = cholesky_pass(block)
    second_basis, second_upper = cholesky_pass(first_basis)
    return (second_basis, multiply(second_upper, first_upper))


def shards(matrix):
    row_count = lax.axis_size("row")
    total_rows = matrix.shape[0] * row_count
    share_rows = PANEL // row_count
    panel = matrix[:, :PANEL]
    local_basis, local_upper = factorize(panel)
    total_gram = lax.psum(multiply(local_upper.T, local_upper), "row")
    whole_upper = jnp.linalg.cholesky(total_gram).T
    change = jax.scipy.linalg.solve_triangular(whole_upper.T, local_upper.T, lower=True).T
    basis = multiply(local_basis, change)
    basis = broadcast(basis, "col", 0)
    full_upper = lax.psum(multiply(basis.T, matrix), "row")
    my_share = lax.dynamic_slice_in_dim(
        full_upper, lax.axis_index("row") * share_rows, share_rows, 0
    )
    projected = matrix - multiply(basis, full_upper)
    scale = jnp.sqrt(jnp.float32(total_rows))
    placed = jnp.concatenate([basis * scale, projected[:, PANEL:]], axis=1)
    reduced = jnp.where(lax.axis_index("col") == 0, placed, projected)
    return (my_share, reduced)


def solution(mesh):
    return jax.shard_map(
        shards,
        mesh=mesh,
        in_specs=(P("row", "col"),),
        out_specs=(P("row", "col"), P("row", "col")),
        check_vma=False,
    )
```

profile of v0, /device:TPU:8, one launch (start us, length us, event | category | flops | bytes accessed | tf_op | source)
XLA Modules:
  0.0 487.8 jit_solution(14583731544222165822)
XLA Ops:
  7.2 5.7 %fusion.7 = f32[256,256]{1,0:T(8,128)S(1)} fusion(f32[2048,2048]{1,0:T(8,128)} %param.4), kind=kOutput, calls=%fused_computation.19 | convolution fusion | flops 1610612736 | bytes 2359296 | tf_op jit(solution)/shard_map/dot_general | solution.py:18
  12.9 3.0 slice_bitcast_fusion
  16.2 11.7 %cholesky.172 = f32[128,128]{1,0:T(8,128)S(1)} custom-call(f32[128,128]{1,0:T(8,128)S(1)} %cholesky.270), custom_call_target="Cholesky" | custom-call | tf_op jit(solution)/shard_map/jit(cholesky)/cholesky | solution.py:23
  27.9 9.8 %custom-call.19 = f32[1,128,128]{1,2,0:T(8,128)S(1)} custom-call(f32[1,128,128]{2,1,0:T(8,128)S(1)} %get-tuple-element.71), custom_call_target="InvertDiagBlocksLowerTriangular" | custom-call | tf_op jit(solution)/shard_map/jit(cholesky)/cholesky | solution.py:23
  38.2 11.9 %cholesky.189 = f32[128,128]{1,0:T(8,128)S(1)} custom-call(f32[128,128]{1,0:T(8,128)S(1)} %convolution_subtract_fusion.6), custom_call_target="Cholesky" | custom-call | tf_op jit(solution)/shard_map/jit(cholesky)/cholesky | solution.py:23
  52.3 4.1 while.6
  56.4 19.7 %custom-call.20 = f32[2,128,128]{1,2,0:T(8,128)S(1)} custom-call(f32[2,128,128]{2,1,0:T(8,128)S(1)} %get-tuple-element.26), custom_call_target="InvertDiagBlocksLowerTriangular" | custom-call | tf_op jit(solution)/shard_map/jit(_solve_triangular)/triangular_solve | solution.py:24
  76.1 2.3 fusion.9
  78.3 3.0 convolution_subtract_fusion.2
  82.5 1.9 fusion
  84.5 11.7 %cholesky.206 = f32[128,128]{1,0:T(8,128)S(1)} custom-call(f32[128,128]{1,0:T(8,128)S(1)} %cholesky.273), custom_call_target="Cholesky" | custom-call | tf_op jit(solution)/shard_map/jit(cholesky)/cholesky | solution.py:23
  96.9 10.2 %custom-call.21 = f32[1,128,128]{1,2,0:T(8,128)S(1)} custom-call(f32[1,128,128]{2,1,0:T(8,128)S(1)} %get-tuple-element.67), custom_call_target="InvertDiagBlocksLowerTriangular" | custom-call | tf_op jit(solution)/shard_map/jit(cholesky)/cholesky | solution.py:23
  107.6 11.7 %cholesky.223 = f32[128,128]{1,0:T(8,128)S(1)} custom-call(f32[128,128]{1,0:T(8,128)S(1)} %convolution_subtract_fusion.5), custom_call_target="Cholesky" | custom-call | tf_op jit(solution)/shard_map/jit(cholesky)/cholesky | solution.py:23
  123.3 4.0 while.7
  128.0 19.8 %custom-call.22 = f32[2,128,128]{1,2,0:T(8,128)S(1)} custom-call(f32[2,128,128]{2,1,0:T(8,128)S(1)} %get-tuple-element.27), custom_call_target="InvertDiagBlocksLowerTriangular" | custom-call | tf_op jit(solution)/shard_map/jit(_solve_triangular)/triangular_solve | solution.py:24
  148.9 1.9 convolution_subtract_fusion.1
  151.9 26.7 %all-reduce.5.cloned.1.call-done = f32[256,256]{0,1:T(8,128)} async-done(((f32[256,256]{0,1:T(8,128)}), f32[256,256]{0,1:T(8,128)}) %all-reduce.5.cloned.1.call-update) | async-done | bytes 262160 | tf_op jit(solution)/shard_map/psum | solution.py:40
  180.7 11.7 %cholesky.240 = f32[128,128]{1,0:T(8,128)S(1)} custom-call(f32[128,128]{1,0:T(8,128)S(1)} %cholesky.276), custom_call_target="Cholesky" | custom-call | tf_op jit(solution)/shard_map/jit(cholesky)/cholesky | solution.py:41
  193.1 9.8 %custom-call.23 = f32[1,128,128]{1,2,0:T(8,128)S(1)} custom-call(f32[1,128,128]{2,1,0:T(8,128)S(1)} %get-tuple-element.63), custom_call_target="InvertDiagBlocksLowerTriangular" | custom-call | tf_op jit(solution)/shard_map/jit(cholesky)/cholesky | solution.py:41
  203.4 11.9 %cholesky.257 = f32[128,128]{1,0:T(8,128)S(1)} custom-call(f32[128,128]{1,0:T(8,128)S(1)} %convolution_subtract_fusion.4), custom_call_target="Cholesky" | custom-call | tf_op jit(solution)/shard_map/jit(cholesky)/cholesky | solution.py:41
  217.5 4.1 while.5
  221.6 19.7 %custom-call.15 = f32[2,128,128]{1,2,0:T(8,128)S(1)} custom-call(f32[2,128,128]{2,1,0:T(8,128)S(1)} %get-tuple-element.19), custom_call_target="InvertDiagBlocksLowerTriangular" | custom-call | tf_op jit(solution)/shard_map/jit(_solve_triangular)/triangular_solve | solution.py:42
  242.3 4.8 convolution_select_fusion
  247.1 84.5 %all-reduce.7.cloned.1.call-done = f32[2048,256]{1,0:T(8,128)} async-done(((f32[2048,256]{1,0:T(8,128)}), f32[2048,256]{1,0:T(8,128)}) %all-reduce.7.cloned.1.call-update) | async-done | bytes 2097168 | tf_op jit(solution)/shard_map/psum | solution.py:14
  331.7 18.6 %fusion.58 = f32[256,2048]{1,0:T(8,128)} fusion(f32[2048,256]{1,0:T(8,128)} %all-reduce.7.cloned.1.call-done, f32[2048,2048]{1,0:T(8,128)} %param.4), kind=kOutput, calls=%fused_computation.107 | convolution fusion | flops 12884901888 | bytes 20971520 | tf_op jit(solution)/shard_map/dot_general | solution.py:18
  350.3 17.9 %copy.7 = f32[2048,2048]{0,1:T(8,128)} copy(f32[2048,2048]{1,0:T(8,128)} %param.4) | data formatting | bytes 33554432 | tf_op args[0]
  369.6 2.9 copy.8
  372.5 39.7 %all-reduce.9.cloned.1.call-done = f32[256,2048]{1,0:T(8,128)} async-done(((f32[256,2048]{1,0:T(8,128)}), f32[256,2048]{1,0:T(8,128)}) %all-reduce.9.cloned.1.call-update) | async-done | bytes 2097168 | tf_op jit(solution)/shard_map/psum | solution.py:45
  412.2 19.5 %convolution_subtract_fusion = f32[2048,2048]{0,1:T(8,128)} fusion(f32[2048,2048]{0,1:T(8,128)} %copy.7, f32[2048,256]{1,0:T(8,128)S(1)} %copy-done, f32[256,2048]{1,0:T(8,128)} %all-reduce.9.cloned.1.call-done), kind=kOutput, calls=%fused_computation.7 | convolution fusion | flops 12889096192 | bytes 37748736 | tf_op jit(solution)/shard_map/dot_general | solution.py:18
  431.7 13.3 %slice.80 = f32[2048,1792]{0,1:T(8,128)} slice(f32[2048,2048]{0,1:T(8,128)} %convolution_subtract_fusion), slice={[0:2048], [256:2048]} | slice | bytes 29360128 | tf_op jit(solution)/shard_map/slice | solution.py:51
  445.0 16.6 %maximum_select_fusion = f32[2048,2048]{0,1:T(8,128)} fusion(f32[2048,2048]{0,1:T(8,128)} %convolution_subtract_fusion, f32[2048,1792]{0,1:T(8,128)} %slice.80, f32[2048,256]{0,1:T(8,128)S(1)} %copy-done.1, pred[]{:T(512)S(6)} %eq.4), kind=kLoop, calls=%fused_computation.6 | loop fusion | flops 8388608 | bytes 50331648 | tf_op jit(solution)/shard_map/jit(_where)/select_n | solution.py:52
  461.5 17.6 %copy.9 = f32[2048,2048]{1,0:T(8,128)} copy(f32[2048,2048]{0,1:T(8,128)} %maximum_select_fusion) | data formatting | bytes 33554432
  (77 shorter events, 29.7 us)
Async XLA Ops:
  7.2 171.4 %all-reduce.5.cloned.1.call-start = ((), (), s32[]{:S(2)}) async-start(), calls=%async_computation | async-start | bytes 524288 | tf_op jit(solution)/shard_map/psum | solution.py:40
  123.2 208.5 %all-reduce.7.cloned.1.call-start = ((), (), s32[]{:S(2)}) async-start(), calls=%async_computation.1 | async-start | bytes 4194304 | tf_op jit(solution)/shard_map/psum | solution.py:14
  127.3 0.7 copy-start.2
  247.1 165.1 %all-reduce.9.cloned.1.call-start = ((), (), s32[]{:S(2)}) async-start(), calls=%async_computation.2 | async-start | bytes 4194304 | tf_op jit(solution)/shard_map/psum | solution.py:45
  350.3 17.9 %copy-start = (f32[2048,256]{1,0:T(8,128)S(1)}, f32[2048,256]{1,0:T(8,128)}, u32[]{:S(2)}) copy-start(f32[2048,256]{1,0:T(8,128)} %all-reduce.7.cloned.1.call-done) | copy-start | bytes 6291460
  431.7 13.3 %copy-start.1 = (f32[2048,256]{0,1:T(8,128)S(1)}, f32[2048,256]{0,1:T(8,128)}, u32[]{:S(2)}) copy-start(f32[2048,256]{0,1:T(8,128)} %copy.8) | copy-start | bytes 6291460
Sparse Core Ops, SparseCore 0:
  123.3 55.2 all-reduce.4
  247.2 84.4 all-reduce.6
  350.4 61.8 all-reduce.8
where the time goes:
time: 497 us; the launch traced here: 488 us
  other arithmetic  182 us (37%)
  waiting for transfers between devices  151 us (30%)
  local copies, waits for them, and re-layouts  70.6 us (14%)
  matrix products  64.9 us (13%)
  between operations  18.4 us (4%)
    psum x1, waiting for transfers between devices, broadcast(): return lax.psum(jnp.where(mine, shard, jnp.zeros_like(shard)), axis)  84.5 us
    another operation x13, other arithmetic, cholesky_pass(): lower = jnp.linalg.cholesky(gram)  69.2 us
    dot_general x7, matrix products, multiply(): jnp.dot(left, right, precision=precise, preferred_element_type=jnp.float32)  52.1 us
    psum x1, waiting for transfers between devices, shards(): full_upper = lax.psum(multiply(basis.T, matrix), 'row')  39.7 us
    another operation x5, other arithmetic, cholesky_pass(): basis = jax.scipy.linalg.solve_triangular(lower, block.T, lower=True).T  39.6 us
    unnamed x8, local copies, waits for them, and re-layouts  36.2 us
    another operation x7, other arithmetic, shards(): whole_upper = jnp.linalg.cholesky(total_gram).T  34.9 us
    psum x1, waiting for transfers between devices, shards(): total_gram = lax.psum(multiply(local_upper.T, local_upper), 'row')  26.7 us
  transfers between devices with their start and end apart: 3, of which 3 were waited for; matrix products, arithmetic and copies ran while one was open for 10% of the time, Pallas kernels for 0%

commit v1 on v0

v1 whole, which is shorter than its diff:
```python
import functools

import jax
import jax.numpy as jnp
from jax import lax
from jax.experimental import pallas as pl
from jax.experimental.pallas import tpu as pltpu
from jax.sharding import PartitionSpec as P

PANEL = 256
BLOCK = 32
CHUNK = 128
TILE = 512
MESH = pl.DeviceIdType.MESH
precise = lax.Precision.HIGHEST


def multiply(left, right, dims=((1,), (0,))):
    return lax.dot_general(
        left, right, (dims, ((), ())), precision=precise, preferred_element_type=jnp.float32
    )


def quick(left, right):
    return jnp.dot(left, right, preferred_element_type=jnp.float32)


def split(value):
    high = value.astype(jnp.bfloat16)
    return high, (value - high.astype(jnp.float32)).astype(jnp.bfloat16)


def factor(work_ref, inverse_ref):
    row_ids = lax.broadcasted_iota(jnp.int32, (PANEL, PANEL), 0)
    col_ids = lax.broadcasted_iota(jnp.int32, (PANEL, PANEL), 1)
    work_ref[:, PANEL:] = (row_ids == col_ids).astype(jnp.float32)

    def step(k, carry):
        first = pl.multiple_of(k * BLOCK, BLOCK)
        rows = work_ref[pl.ds(first, BLOCK), :]
        picks_row = lax.broadcasted_iota(jnp.int32, (PANEL, 128), 0)
        picks_col = lax.broadcasted_iota(jnp.int32, (PANEL, 128), 1)
        picks = ((picks_row == picks_col + first) & (picks_col < BLOCK)).astype(jnp.float32)
        left = multiply(rows[:, :PANEL], picks)
        row = lax.broadcasted_iota(jnp.int32, (BLOCK, 128), 0)
        col = lax.broadcasted_iota(jnp.int32, (BLOCK, 128), 1)
        right = (row == col).astype(jnp.float32)
        for j in range(BLOCK):
            pivot = left[j : j + 1, j : j + 1]
            inv = lax.rsqrt(pivot)
            inv = inv * (1.5 - 0.5 * pivot * inv * inv)
            left_row = left[j : j + 1, :] * inv
            right_row = right[j : j + 1, :] * inv
            column = jnp.where(row > j, left[:, j : j + 1] * inv, 0.0)
            left = left - column * left_row
            right = jnp.where(row == j, right_row, right - column * right_row)
        solved = multiply(right[:, :BLOCK], rows)
        work_ref[pl.ds(first, BLOCK), :] = solved
        change = multiply(solved[:, :PANEL], solved, ((0,), (0,)))
        below = lax.broadcasted_iota(jnp.int32, (PANEL, 2 * PANEL), 0) >= first + BLOCK
        whole = work_ref[...]
        work_ref[...] = jnp.where(below, whole - change, whole)
        return carry

    lax.fori_loop(0, PANEL // BLOCK, step, 0)
    inverse_ref[...] = work_ref[:, PANEL:]


def gather_kernel(
    row_n,
    col_n,
    matrix_ref,
    panel_ref,
    inverse_ref,
    total_ref,
    products_ref,
    held_ref,
    gram_ref,
    gram_in_ref,
    work_ref,
    sums_in_ref,
    load_sem,
    panel_sem,
    chunk_send,
    chunk_recv,
    gram_send,
    gram_recv,
    inv_send,
    inv_recv,
    rs_send,
    rs_recv,
    ag_send,
    ag_recv,
):
    r = lax.axis_index("row")
    z = lax.axis_index("col")
    rows, cols = held_ref.shape
    chunks = rows // CHUNK
    half = chunks // 2
    blocks = rows // PANEL
    per_block = PANEL // CHUNK
    levels = row_n.bit_length() - 1

    parity = lax.rem(r, 2)
    bits = []
    for s in range(levels):
        even = 1 << s
        odd = 1 if s == 0 else 1 << (levels - s)
        bits.append(even + parity * (odd - even))
    mine = [lax.rem(lax.div(r, bit), 2) for bit in bits]
    partner = [r + bit * (1 - 2 * own) for bit, own in zip(bits, mine)]

    panel_load = pltpu.make_async_copy(
        matrix_ref.at[:, pl.ds(0, PANEL)], panel_ref, panel_sem
    )

    @pl.when(z == 0)
    def _():
        panel_load.start()

    def load(i):
        span = pl.ds(pl.multiple_of(i * PANEL, PANEL), PANEL)
        return pltpu.make_async_copy(matrix_ref.at[span, :], held_ref.at[span, :], load_sem.at[i])

    for i in range(blocks):
        load(i).start()

    barrier = pltpu.get_barrier_semaphore()
    for other in partner:
        pl.semaphore_signal(
            barrier, inc=1, device_id={"row": other, "col": z}, device_id_type=MESH
        )
    for d in range(1, col_n):
        pl.semaphore_signal(
            barrier,
            inc=1,
            device_id={"row": r, "col": lax.rem(z + d, col_n)},
            device_id_type=MESH,
        )
    products_ref[...] = jnp.zeros_like(products_ref)
    pl.semaphore_wait(barrier, levels + col_n - 1)

    def send_chunk(i, to):
        span = pl.ds(pl.multiple_of(i * CHUNK, CHUNK), CHUNK)
        return pltpu.make_async_remote_copy(
            src_ref=panel_ref.at[span, :],
            dst_ref=panel_ref.at[span, :],
            send_sem=chunk_send.at[i],
            recv_sem=chunk_recv.at[i],
            device_id={"row": r, "col": to},
            device_id_type=MESH,
        )

    up = lax.rem(z + 1, col_n)
    down = lax.rem(z + col_n - 1, col_n)

    def add_block(i):
        load(i).wait()
        span = pl.ds(pl.multiple_of(i * PANEL, PANEL), PANEL)
        high, low = split(panel_ref[span, :].T)
        for c in range(0, cols, TILE):
            m_high, m_low = split(held_ref[span, pl.ds(c, TILE)])
            products_ref[:, pl.ds(c, TILE)] += (
                quick(high, m_high) + quick(high, m_low) + quick(low, m_high)
            )

    def send_inverse(d):
        return pltpu.make_async_remote_copy(
            src_ref=inverse_ref,
            dst_ref=inverse_ref,
            send_sem=inv_send.at[d - 1],
            recv_sem=inv_recv,
            device_id={"row": r, "col": lax.rem(z + d, col_n)},
            device_id_type=MESH,
        )

    @pl.when(z == 0)
    def _():
        panel_load.wait()
        for i in range(half):
            send_chunk(i, up).start()
            send_chunk(half + i, down).start()
        gram_ref[...] = jnp.zeros_like(gram_ref)

        def gram_block(i, carry):
            part = panel_ref[pl.ds(pl.multiple_of(i * PANEL, PANEL), PANEL), :]
            gram_ref[...] += multiply(part, part, ((0,), (0,)))
            return carry

        lax.fori_loop(0, blocks, gram_block, 0)
        for s in range(levels):
            copy = pltpu.make_async_remote_copy(
                src_ref=gram_ref,
                dst_ref=gram_in_ref.at[s],
                send_sem=gram_send.at[s],
                recv_sem=gram_recv.at[s],
                device_id={"row": partner[s], "col": z},
                device_id_type=MESH,
            )
            copy.start()

            def filler(i, carry):
                add_block(i)
                return carry

            lax.fori_loop(blocks * s // levels, blocks * (s + 1) // levels, filler, 0)
            copy.wait()
            gram_ref[...] += gram_in_ref[s]
        work_ref[:, :PANEL] = gram_ref[...]
        factor(work_ref, inverse_ref)
        for d in range(1, col_n):
            send_inverse(d).start()

    @pl.when(z > 0)
    def _():
        def slot(t, carry):
            one = t - z
            two = t - (col_n - z)

            @pl.when((one >= 0) & (one < half))
            def _():
                copy = send_chunk(one, up)
                copy.wait_recv()

                @pl.when(z < col_n - 1)
                def _():
                    copy.start()

            @pl.when((two >= 0) & (two < half))
            def _():
                copy = send_chunk(half + two, down)
                copy.wait_recv()

                @pl.when(z > 1)
                def _():
                    copy.start()

            @pl.when((one >= 0) & (one < half) & (lax.rem(one + per_block, per_block) == per_block - 1))
            def _():
                add_block(lax.div(one, per_block))

            @pl.when((two >= 0) & (two < half) & (lax.rem(two + per_block, per_block) == per_block - 1))
            def _():
                add_block(lax.div(half + two, per_block))

            return carry

        lax.fori_loop(1, half + col_n - 1, slot, 0)

    low = 0
    size = PANEL
    offset = 0
    spans = []
    for s in range(levels):
        size //= 2
        keep = pl.multiple_of(low + mine[s] * size, size)
        give = pl.multiple_of(low + (1 - mine[s]) * size, size)
        copy = pltpu.make_async_remote_copy(
            src_ref=products_ref.at[pl.ds(give, size), :],
            dst_ref=sums_in_ref.at[pl.ds(offset, size), :],
            send_sem=rs_send.at[s],
            recv_sem=rs_recv.at[s],
            device_id={"row": partner[s], "col": z},
            device_id_type=MESH,
        )
        copy.start()
        copy.wait()
        summed_ref = total_ref if s == levels - 1 else products_ref
        summed_ref[pl.ds(keep, size), :] = (
            products_ref[pl.ds(keep, size), :] + sums_in_ref[pl.ds(offset, size), :]
        )
        spans.append((keep, size))
        low = keep
        offset += size
    for s in reversed(range(levels)):
        keep, size = spans[s]
        span = pl.ds(keep, size)
        copy = pltpu.make_async_remote_copy(
            src_ref=total_ref.at[span, :],
            dst_ref=total_ref.at[span, :],
            send_sem=ag_send.at[s],
            recv_sem=ag_recv.at[s],
            device_id={"row": partner[s], "col": z},
            device_id_type=MESH,
        )
        copy.start()
        copy.wait()

    @pl.when(z == 0)
    def _():
        for d in range(1, col_n):
            send_inverse(d).wait_send()

    @pl.when(z > 0)
    def _():
        send_inverse(1).wait_recv()

    def drain(i, carry):
        @pl.when(z < col_n - 1)
        def _():
            send_chunk(i, up).wait_send()

        @pl.when(z != 1)
        def _():
            send_chunk(half + i, down).wait_send()

        return carry

    lax.fori_loop(0, half, drain, 0)


def project_kernel(
    total_rows, share_rows, matrix_ref, panel_ref, inverse_ref, products_ref,
    share_ref, reduced_ref, high_ref, low_ref,
):
    r = lax.axis_index("row")
    z = lax.axis_index("col")
    cols = matrix_ref.shape[1]

    @pl.when(pl.program_id(0) == 0)
    def _():
        for c in range(0, cols, TILE):
            upper = multiply(inverse_ref[...], products_ref[:, pl.ds(c, TILE)])
            high_ref[:, pl.ds(c, TILE)], low_ref[:, pl.ds(c, TILE)] = split(upper)
        mine = pl.ds(pl.multiple_of(r * share_rows, share_rows), share_rows)
        for c in range(0, cols, TILE):
            share_ref[:, pl.ds(c, TILE)] = multiply(
                inverse_ref[mine, :], products_ref[:, pl.ds(c, TILE)]
            )

    basis = multiply(panel_ref[...], inverse_ref[...], ((1,), (1,)))
    high, low = split(basis)
    for c in range(0, cols, TILE):
        u_high = high_ref[:, pl.ds(c, TILE)]
        reduced_ref[:, pl.ds(c, TILE)] = matrix_ref[:, pl.ds(c, TILE)] - (
            quick(high, u_high) + quick(high, low_ref[:, pl.ds(c, TILE)]) + quick(low, u_high)
        )

    @pl.when(z == 0)
    def _():
        reduced_ref[:, :PANEL] = basis * (total_rows**0.5)


def shards(matrix):
    row_n = lax.axis_size("row")
    col_n = lax.axis_size("col")
    rows, cols = matrix.shape
    levels = row_n.bit_length() - 1
    chunks = rows // CHUNK
    dma = pltpu.SemaphoreType.DMA
    vmem = pl.BlockSpec(memory_space=pltpu.VMEM)
    panel, inverse, products = pl.pallas_call(
        functools.partial(gather_kernel, row_n, col_n),
        out_shape=(
            jax.ShapeDtypeStruct((rows, PANEL), jnp.float32),
            jax.ShapeDtypeStruct((PANEL, PANEL), jnp.float32),
            jax.ShapeDtypeStruct((PANEL, cols), jnp.float32),
        ),
        in_specs=[pl.BlockSpec(memory_space=pl.ANY)],
        out_specs=(vmem, vmem, vmem),
        scratch_shapes=[
            pltpu.VMEM((PANEL, cols), jnp.float32),
            pltpu.VMEM((rows, cols), jnp.float32),
            pltpu.VMEM((PANEL, PANEL), jnp.float32),
            pltpu.VMEM((levels, PANEL, PANEL), jnp.float32),
            pltpu.VMEM((PANEL, 2 * PANEL), jnp.float32),
            pltpu.VMEM((PANEL, cols), jnp.float32),
            dma((rows // PANEL,)),
            dma,
            dma((chunks,)),
            dma((chunks,)),
            dma((levels,)),
            dma((levels,)),
            dma((col_n,)),
            dma,
            dma((levels,)),
            dma((levels,)),
            dma((levels,)),
            dma((levels,)),
        ],
        compiler_params=pltpu.CompilerParams(
            collective_id=0, has_side_effects=True, vmem_limit_bytes=48 * 1024 * 1024
        ),
        name="gather",
    )(matrix)
    share_rows = PANEL // row_n
    return tuple(
        pl.pallas_call(
            functools.partial(project_kernel, rows * row_n, share_rows),
            grid=(rows // PANEL,),
            out_shape=(
                jax.ShapeDtypeStruct((share_rows, cols), jnp.float32),
                jax.ShapeDtypeStruct((rows, cols), jnp.float32),
            ),
            in_specs=[
                pl.BlockSpec((PANEL, cols), lambda i: (i, 0)),
                pl.BlockSpec((PANEL, PANEL), lambda i: (i, 0)),
                pl.BlockSpec((PANEL, PANEL), lambda i: (0, 0)),
                pl.BlockSpec((PANEL, cols), lambda i: (0, 0)),
            ],
            out_specs=(
                pl.BlockSpec((share_rows, cols), lambda i: (0, 0)),
                pl.BlockSpec((PANEL, cols), lambda i: (i, 0)),
            ),
            scratch_shapes=[
                pltpu.VMEM((PANEL, cols), jnp.bfloat16),
                pltpu.VMEM((PANEL, cols), jnp.bfloat16),
            ],
            compiler_params=pltpu.CompilerParams(vmem_limit_bytes=40 * 1024 * 1024),
            name="project",
        )(matrix, panel, inverse, products)
    )


def solution(mesh):
    return jax.shard_map(
        shards,
        mesh=mesh,
        in_specs=(P("row", "col"),),
        out_specs=(P("row", "col"), P("row", "col")),
        check_vma=False,
    )
```

time: 497 us -> 120 us (0.24)
  the two profiles are of different devices: /device:TPU:8 before, /device:TPU:15 now
where the time goes in v1:
time: 120 us; the launch traced here: 119 us
  Pallas kernels  119 us (99%)
    pallas_call x1, Pallas kernels, shards(): pl.pallas_call(functools.partial(gather_kernel, row_n, col_n), out_shape=...  96.6 us
    pallas_call x1, Pallas kernels, shards(): pl.pallas_call(functools.partial(project_kernel, rows * row_n, share_rows...  22.1 us

profile of v1, /device:TPU:15, one launch (start us, length us, event | category | flops | bytes accessed | tf_op | source)
XLA Modules:
  0.0 119.3 jit_solution(6940371769112297325)
XLA Ops:
  0.6 96.6 %gather.1 = (f32[2048,256]{1,0:T(8,128)S(1)}, f32[256,256]{1,0:T(8,128)S(1)}, f32[256,2048]{1,0:T(8,128)S(1)}) custom-call(f32[2048,2048]{1,0:T(8,128)} %matrix_ref.3), custom_call_target="tpu_custom_call" | custom-call | tf_op jit(solution)/shard_map/gather/pallas_call | solution.py:352
  97.2 22.1 %project.1 = (f32[32,2048]{1,0:T(8,128)}, f32[2048,2048]{1,0:T(8,128)}) custom-call(f32[2048,2048]{1,0:T(8,128)} %matrix_ref.3, f32[2048,256]{1,0:T(8,128)S(1)} %get-tuple-element.5.panel_ref, f32[256,256]{1,0:T(8,128)S(1)} %get-tuple-element.6.inverse_ref, f32[256,2048]{1,0:T(8,128)S(1)} %get-tuple-element.7.products_ref), custom_call_target="tpu_custom_call" | custom-call | tf_op jit(solution)/shard_map/project/pallas_call | solution.py:388

commit v2 on v1

v2 whole, which is shorter than its diff:
```python
import functools

import jax
import jax.numpy as jnp
from jax import lax
from jax.experimental import pallas as pl
from jax.experimental.pallas import tpu as pltpu
from jax.sharding import PartitionSpec as P

PANEL = 256
LANES = 128
BLOCK = 32
CHUNK = 256
TILE = 512
MESH = pl.DeviceIdType.MESH
precise = lax.Precision.HIGHEST


def multiply(left, right, dims=((1,), (0,))):
    return lax.dot_general(
        left, right, (dims, ((), ())), precision=precise, preferred_element_type=jnp.float32
    )


def quick(left, right):
    return jnp.dot(left, right, preferred_element_type=jnp.float32)


def split(value):
    high = value.astype(jnp.bfloat16)
    return high, (value - high.astype(jnp.float32)).astype(jnp.bfloat16)


def factor(work_ref, inverse_ref, between):
    row_ids = lax.broadcasted_iota(jnp.int32, (PANEL, PANEL), 0)
    col_ids = lax.broadcasted_iota(jnp.int32, (PANEL, PANEL), 1)
    work_ref[:, PANEL:] = (row_ids == col_ids).astype(jnp.float32)

    def step(k, carry):
        between(k)
        first = pl.multiple_of(k * BLOCK, BLOCK)
        rows = work_ref[pl.ds(first, BLOCK), :]
        picks_row = lax.broadcasted_iota(jnp.int32, (PANEL, 128), 0)
        picks_col = lax.broadcasted_iota(jnp.int32, (PANEL, 128), 1)
        picks = ((picks_row == picks_col + first) & (picks_col < BLOCK)).astype(jnp.float32)
        left = multiply(rows[:, :PANEL], picks)
        row = lax.broadcasted_iota(jnp.int32, (BLOCK, 128), 0)
        col = lax.broadcasted_iota(jnp.int32, (BLOCK, 128), 1)
        right = (row == col).astype(jnp.float32)
        for j in range(BLOCK):
            pivot = left[j : j + 1, j : j + 1]
            inv = lax.rsqrt(pivot)
            inv = inv * (1.5 - 0.5 * pivot * inv * inv)
            left_row = left[j : j + 1, :] * inv
            right_row = right[j : j + 1, :] * inv
            column = jnp.where(row > j, left[:, j : j + 1] * inv, 0.0)
            left = left - column * left_row
            right = jnp.where(row == j, right_row, right - column * right_row)
        solved = multiply(right[:, :BLOCK], rows)
        work_ref[pl.ds(first, BLOCK), :] = solved
        change = multiply(solved[:, :PANEL], solved, ((0,), (0,)))
        below = lax.broadcasted_iota(jnp.int32, (PANEL, 2 * PANEL), 0) >= first + BLOCK
        whole = work_ref[...]
        work_ref[...] = jnp.where(below, whole - change, whole)
        return carry

    lax.fori_loop(0, PANEL // BLOCK, step, 0)
    inverse_ref[...] = work_ref[:, PANEL:]


def gather_kernel(
    row_n,
    col_n,
    matrix_ref,
    panel_ref,
    inverse_ref,
    total_ref,
    held_ref,
    products_ref,
    gram_ref,
    gram_in_ref,
    work_ref,
    sums_in_ref,
    load_sem,
    panel_sem,
    chunk_send,
    chunk_recv,
    gram_send,
    gram_recv,
    inv_send,
    inv_recv,
    sum_send,
    sum_recv,
):
    r = lax.axis_index("row")
    z = lax.axis_index("col")
    rows, cols = held_ref.shape
    pieces = PANEL // LANES
    blocks = rows // CHUNK
    chunks = pieces * blocks
    levels = row_n.bit_length() - 1
    stages = 2 * levels

    parity = lax.rem(r, 2)
    bits = []
    for s in range(levels):
        even = 1 << s
        odd = 1 if s == 0 else 1 << (levels - s)
        bits.append(even + parity * (odd - even))
    mine = [lax.rem(lax.div(r, bit), 2) for bit in bits]
    partner = [r + bit * (1 - 2 * own) for bit, own in zip(bits, mine)]

    def span_of(i):
        return pl.ds(pl.multiple_of(i * CHUNK, CHUNK), CHUNK)

    def load(i):
        return pltpu.make_async_copy(
            matrix_ref.at[span_of(i), :], held_ref.at[span_of(i), :], load_sem.at[i]
        )

    def load_chunk(c):
        p, i = c // blocks, c % blocks
        return pltpu.make_async_copy(
            matrix_ref.at[span_of(i), pl.ds(p * LANES, LANES)],
            panel_ref.at[p, span_of(i), :],
            panel_sem.at[c],
        )

    @pl.when(z == 0)
    def _():
        for c in range(chunks):
            load_chunk(c).start()

    @pl.when(z > 0)
    def _():
        for i in range(blocks):
            load(i).start()

    barrier = pltpu.get_barrier_semaphore()
    for other in partner:
        pl.semaphore_signal(
            barrier, inc=1, device_id={"row": other, "col": z}, device_id_type=MESH
        )
    for d in range(1, col_n):
        pl.semaphore_signal(
            barrier,
            inc=1,
            device_id={"row": r, "col": lax.rem(z + d, col_n)},
            device_id_type=MESH,
        )
    pl.semaphore_wait(barrier, levels + col_n - 1)

    def send_chunk(c):
        p = lax.div(c, blocks)
        span = span_of(lax.rem(c, blocks))
        return pltpu.make_async_remote_copy(
            src_ref=panel_ref.at[p, span, :],
            dst_ref=panel_ref.at[p, span, :],
            send_sem=chunk_send.at[c],
            recv_sem=chunk_recv.at[c],
            device_id={"row": r, "col": lax.rem(z + 1, col_n)},
            device_id_type=MESH,
        )

    def add_block(c):
        p = lax.div(c, blocks)
        i = lax.rem(c, blocks)

        @pl.when(c < blocks)
        def _():
            load(i).wait()

        high, low = split(panel_ref[p, span_of(i), :].T)
        both = jnp.concatenate([high, low], axis=0)
        for t in range(0, cols, TILE):
            m_high, m_low = split(held_ref[span_of(i), pl.ds(t, TILE)])
            with_high = quick(both, m_high)
            products_ref[p, :, pl.ds(t, TILE)] += (
                with_high[:LANES] + with_high[LANES:] + quick(high, m_low)
            )

    def send_inverse(d):
        return pltpu.make_async_remote_copy(
            src_ref=inverse_ref,
            dst_ref=inverse_ref,
            send_sem=inv_send.at[d - 1],
            recv_sem=inv_recv,
            device_id={"row": r, "col": lax.rem(z + d, col_n)},
            device_id_type=MESH,
        )

    keeps, gives, sizes, offsets = [], [], [], []
    low_row, size, offset = 0, LANES, 0
    for s in range(levels):
        size //= 2
        keeps.append(pl.multiple_of(low_row + mine[s] * size, size))
        gives.append(pl.multiple_of(low_row + (1 - mine[s]) * size, size))
        sizes.append(size)
        offsets.append(offset)
        low_row = keeps[-1]
        offset += size

    def stage(p, s):
        level = s if s < levels else stages - 1 - s
        size = sizes[level]
        if s < levels:
            src = products_ref.at[p, pl.ds(gives[level], size), :]
            dst = sums_in_ref.at[p, pl.ds(offsets[level], size), :]
        else:
            src = dst = total_ref.at[p, pl.ds(keeps[level], size), :]
        return pltpu.make_async_remote_copy(
            src_ref=src,
            dst_ref=dst,
            send_sem=sum_send.at[p, s],
            recv_sem=sum_recv.at[p, s],
            device_id={"row": partner[level], "col": z},
            device_id_type=MESH,
        )

    def advance(p, s):
        if s > 0:
            stage(p, s - 1).wait()
            if s <= levels:
                span = pl.ds(keeps[s - 1], sizes[s - 1])
                arrived = pl.ds(offsets[s - 1], sizes[s - 1])
                summed_ref = total_ref if s == levels else products_ref
                summed_ref[p, span, :] = products_ref[p, span, :] + sums_in_ref[p, arrived, :]
        if s < stages:
            stage(p, s).start()

    @pl.when(z == 0)
    def _():
        for c in range(chunks):
            load_chunk(c).wait()
            send_chunk(c).start()
        for i in range(blocks):
            load(i).start()
        products_ref[...] = jnp.zeros_like(products_ref)
        gram_ref[...] = jnp.zeros_like(gram_ref)

        def gram_block(i, carry):
            part = jnp.concatenate([panel_ref[p, span_of(i), :] for p in range(pieces)], axis=1)
            gram_ref[...] += multiply(part, part, ((0,), (0,)))
            return carry

        lax.fori_loop(0, blocks, gram_block, 0)

        def filler(c, carry):
            add_block(c)
            return carry

        for s in range(levels):
            copy = pltpu.make_async_remote_copy(
                src_ref=gram_ref,
                dst_ref=gram_in_ref.at[s],
                send_sem=gram_send.at[s],
                recv_sem=gram_recv.at[s],
                device_id={"row": partner[s], "col": z},
                device_id_type=MESH,
            )
            copy.start()
            lax.fori_loop(chunks * s // levels, chunks * (s + 1) // levels, filler, 0)
            copy.wait()
            gram_ref[...] += gram_in_ref[s]
        work_ref[:, :PANEL] = gram_ref[...]
        steps = PANEL // BLOCK
        inside = min(steps, stages + 1)

        def between(k):
            for s in range(inside):

                @pl.when(k == s)
                def _():
                    for p in range(pieces):
                        advance(p, s)

        factor(work_ref, inverse_ref, between)
        for d in range(1, col_n):
            send_inverse(d).start()
        for s in range(inside, stages + 1):
            for p in range(pieces):
                advance(p, s)
        for d in range(1, col_n):
            send_inverse(d).wait_send()

    @pl.when(z > 0)
    def _():
        products_ref[...] = jnp.zeros_like(products_ref)
        inside = min(blocks, stages + 1)

        def slot(c, carry):
            copy = send_chunk(c)
            copy.wait_recv()

            @pl.when(z < col_n - 1)
            def _():
                copy.start()

            for p in range(pieces - 1):
                for s in range(inside):

                    @pl.when(c == (p + 1) * blocks + s)
                    def _():
                        advance(p, s)

            add_block(c)
            return carry

        lax.fori_loop(0, chunks, slot, 0)
        for p in range(pieces - 1):
            for s in range(inside, stages + 1):
                advance(p, s)
        for s in range(stages + 1):
            advance(pieces - 1, s)
        send_inverse(1).wait_recv()

    def drain(c, carry):
        @pl.when(z < col_n - 1)
        def _():
            send_chunk(c).wait_send()

        return carry

    lax.fori_loop(0, chunks, drain, 0)


def project_kernel(
    total_rows, share_rows, matrix_ref, panel_ref, inverse_ref, products_ref,
    share_ref, reduced_ref, high_ref, low_ref,
):
    r = lax.axis_index("row")
    z = lax.axis_index("col")
    cols = matrix_ref.shape[1]
    pieces = PANEL // LANES

    @pl.when(pl.program_id(0) == 0)
    def _():
        mine = pl.ds(pl.multiple_of(r * share_rows, share_rows), share_rows)
        for t in range(0, cols, TILE):
            tile = pl.ds(t, TILE)
            products = jnp.concatenate([products_ref[p, :, tile] for p in range(pieces)], axis=0)
            upper = multiply(inverse_ref[...], products)
            high_ref[:, tile], low_ref[:, tile] = split(upper)
            share_ref[:, tile] = multiply(inverse_ref[mine, :], products)

    rows = pl.ds(pl.multiple_of(pl.program_id(0) * PANEL, PANEL), PANEL)
    panel = jnp.concatenate([panel_ref[p, rows, :] for p in range(pieces)], axis=1)
    basis = multiply(panel, inverse_ref[...], ((1,), (1,)))
    high, low = split(basis)
    both = jnp.concatenate([high, low], axis=0)
    for t in range(0, cols, TILE):
        tile = pl.ds(t, TILE)
        with_high = quick(both, high_ref[:, tile])
        reduced_ref[:, tile] = matrix_ref[rows, tile] - (
            with_high[:PANEL] + with_high[PANEL:] + quick(high, low_ref[:, tile])
        )

    @pl.when(z == 0)
    def _():
        reduced_ref[:, :PANEL] = basis * (total_rows**0.5)


def shards(matrix):
    row_n = lax.axis_size("row")
    col_n = lax.axis_size("col")
    rows, cols = matrix.shape
    levels = row_n.bit_length() - 1
    pieces = PANEL // LANES
    blocks = rows // CHUNK
    chunks = pieces * blocks
    dma = pltpu.SemaphoreType.DMA
    vmem = pl.BlockSpec(memory_space=pltpu.VMEM)
    panel, inverse, products, held = pl.pallas_call(
        functools.partial(gather_kernel, row_n, col_n),
        out_shape=(
            jax.ShapeDtypeStruct((pieces, rows, LANES), jnp.float32),
            jax.ShapeDtypeStruct((PANEL, PANEL), jnp.float32),
            jax.ShapeDtypeStruct((pieces, LANES, cols), jnp.float32),
            jax.ShapeDtypeStruct((rows, cols), jnp.float32),
        ),
        in_specs=[pl.BlockSpec(memory_space=pl.ANY)],
        out_specs=(vmem, vmem, vmem, vmem),
        scratch_shapes=[
            pltpu.VMEM((pieces, LANES, cols), jnp.float32),
            pltpu.VMEM((PANEL, PANEL), jnp.float32),
            pltpu.VMEM((levels, PANEL, PANEL), jnp.float32),
            pltpu.VMEM((PANEL, 2 * PANEL), jnp.float32),
            pltpu.VMEM((pieces, LANES, cols), jnp.float32),
            dma((blocks,)),
            dma((chunks,)),
            dma((chunks,)),
            dma((chunks,)),
            dma((levels,)),
            dma((levels,)),
            dma((col_n,)),
            dma,
            dma((pieces, 2 * levels)),
            dma((pieces, 2 * levels)),
        ],
        compiler_params=pltpu.CompilerParams(
            collective_id=0, has_side_effects=True, vmem_limit_bytes=32 * 1024 * 1024
        ),
        name="gather",
    )(matrix)
    share_rows = PANEL // row_n
    return tuple(
        pl.pallas_call(
            functools.partial(project_kernel, rows * row_n, share_rows),
            grid=(rows // PANEL,),
            out_shape=(
                jax.ShapeDtypeStruct((share_rows, cols), jnp.float32),
                jax.ShapeDtypeStruct((rows, cols), jnp.float32),
            ),
            in_specs=[vmem, vmem, vmem, vmem],
            out_specs=(
                pl.BlockSpec((share_rows, cols), lambda i: (0, 0)),
                pl.BlockSpec((PANEL, cols), lambda i: (i, 0)),
            ),
            scratch_shapes=[
                pltpu.VMEM((PANEL, cols), jnp.bfloat16),
                pltpu.VMEM((PANEL, cols), jnp.bfloat16),
            ],
            compiler_params=pltpu.CompilerParams(vmem_limit_bytes=24 * 1024 * 1024),
            name="project",
        )(held, panel, inverse, products)
    )


def solution(mesh):
    return jax.shard_map(
        shards,
        mesh=mesh,
        in_specs=(P("row", "col"),),
        out_specs=(P("row", "col"), P("row", "col")),
        check_vma=False,
    )
```

time: 120 us -> 109 us (0.908)
  the two profiles are of different devices: /device:TPU:15 before, /device:TPU:27 now
where the time goes in v2:
time: 109 us
  Pallas kernels  109 us (100%)
    pallas_call x1, Pallas kernels, shards(): pl.pallas_call(functools.partial(gather_kernel, row_n, col_n), out_shape=...  90.3 us
    pallas_call x1, Pallas kernels, shards(): pl.pallas_call(functools.partial(project_kernel, rows * row_n, share_rows...  18.3 us

profile of v2, /device:TPU:27, one launch (start us, length us, event | category | flops | bytes accessed | tf_op | source)
XLA Modules:
  0.0 109.2 jit_solution(9386990430112351605)
XLA Ops:
  0.6 90.3 %gather.1 = (f32[2,2048,128]{2,1,0:T(8,128)S(1)}, f32[256,256]{1,0:T(8,128)S(1)}, f32[2,128,2048]{2,1,0:T(8,128)S(1)}, f32[2048,2048]{1,0:T(8,128)S(1)}) custom-call(f32[2048,2048]{1,0:T(8,128)} %matrix_ref.1), custom_call_target="tpu_custom_call" | custom-call | tf_op jit(solution)/shard_map/gather/pallas_call | solution.py:373
  90.9 18.3 %project.1 = (f32[32,2048]{1,0:T(8,128)}, f32[2048,2048]{1,0:T(8,128)}) custom-call(f32[2048,2048]{1,0:T(8,128)S(1)} %get-tuple-element.6.matrix_ref, f32[2,2048,128]{2,1,0:T(8,128)S(1)} %get-tuple-element.7.panel_ref, f32[256,256]{1,0:T(8,128)S(1)} %get-tuple-element.8.inverse_ref, f32[2,128,2048]{2,1,0:T(8,128)S(1)} %get-tuple-element.9.products_ref), custom_call_target="tpu_custom_call" | custom-call | tf_op jit(solution)/shard_map/project/pallas_call | solution.py:407

commit v3 on v2

--- a/solution.py
+++ b/solution.py
@@ -11,6 +11,7 @@
 LANES = 128
 BLOCK = 32
 CHUNK = 256
+SENT = 128
 TILE = 512
 MESH = pl.DeviceIdType.MESH
 precise = lax.Precision.HIGHEST
@@ -151,8 +152,9 @@
     pl.semaphore_wait(barrier, levels + col_n - 1)
 
     def send_chunk(c):
-        p = lax.div(c, blocks)
-        span = span_of(lax.rem(c, blocks))
+        per_piece = rows // SENT
+        p = lax.div(c, per_piece)
+        span = pl.ds(pl.multiple_of(lax.rem(c, per_piece) * SENT, SENT), SENT)
         return pltpu.make_async_remote_copy(
             src_ref=panel_ref.at[p, span, :],
             dst_ref=panel_ref.at[p, span, :],
@@ -232,7 +234,8 @@
     def _():
         for c in range(chunks):
             load_chunk(c).wait()
-            send_chunk(c).start()
+            for h in range(CHUNK // SENT):
+                send_chunk(c * (CHUNK // SENT) + h).start()
         for i in range(blocks):
             load(i).start()
         products_ref[...] = jnp.zeros_like(products_ref)
@@ -244,6 +247,8 @@
             return carry
 
         lax.fori_loop(0, blocks, gram_block, 0)
+
+        early = (pieces - 1) * blocks
 
         def filler(c, carry):
             add_block(c)
@@ -259,7 +264,7 @@
                 device_id_type=MESH,
             )
             copy.start()
-            lax.fori_loop(chunks * s // levels, chunks * (s + 1) // levels, filler, 0)
+            lax.fori_loop(early * s // levels, early * (s + 1) // levels, filler, 0)
             copy.wait()
             gram_ref[...] += gram_in_ref[s]
         work_ref[:, :PANEL] = gram_ref[...]
@@ -271,17 +276,16 @@
 
                 @pl.when(k == s)
                 def _():
-                    for p in range(pieces):
+                    for p in range(pieces - 1):
                         advance(p, s)
 
         factor(work_ref, inverse_ref, between)
         for d in range(1, col_n):
             send_inverse(d).start()
         for s in range(inside, stages + 1):
-            for p in range(pieces):
+            for p in range(pieces - 1):
                 advance(p, s)
-        for d in range(1, col_n):
-            send_inverse(d).wait_send()
+        lax.fori_loop(early, chunks, filler, 0)
 
     @pl.when(z > 0)
     def _():
@@ -289,12 +293,10 @@
         inside = min(blocks, stages + 1)
 
         def slot(c, carry):
-            copy = send_chunk(c)
-            copy.wait_recv()
-
-            @pl.when(z < col_n - 1)
-            def _():
-                copy.start()
+            for h in range(CHUNK // SENT):
+                copy = send_chunk(c * (CHUNK // SENT) + h)
+                copy.wait_recv()
+                pl.when(z < col_n - 1)(copy.start)
 
             for p in range(pieces - 1):
                 for s in range(inside):
@@ -310,18 +312,33 @@
         for p in range(pieces - 1):
             for s in range(inside, stages + 1):
                 advance(p, s)
-        for s in range(stages + 1):
-            advance(pieces - 1, s)
-        send_inverse(1).wait_recv()
 
     def drain(c, carry):
-        @pl.when(z < col_n - 1)
-        def _():
-            send_chunk(c).wait_send()
-
+        pl.when(z < col_n - 1)(send_chunk(c).wait_send)
         return carry
 
-    lax.fori_loop(0, chunks, drain, 0)
+    def form_basis(i, carry):
+        block = jnp.concatenate([panel_ref[p, span_of(i), :] for p in range(pieces)], axis=1)
+        basis = multiply(block, inverse_ref[...], ((1,), (1,)))
+        for p in range(pieces):
+            panel_ref[p, span_of(i), :] = basis[:, p * LANES : (p + 1) * LANES]
+        return carry
+
+    for s in range(stages + 1):
+        advance(pieces - 1, s)
+        if s == levels:
+            lax.fori_loop(0, chunks * CHUNK // SENT, drain, 0)
+            pl.when(z > 0)(send_inverse(1).wait_recv)
+        if levels <= s < stages:
+            done = s - levels
+            lax.fori_loop(
+                blocks * done // levels, blocks * (done + 1) // levels, form_basis, 0
+            )
+
+    @pl.when(z == 0)
+    def _():
+        for d in range(1, col_n):
+            send_inverse(d).wait_send()
 
 
 def project_kernel(
@@ -344,8 +361,7 @@
             share_ref[:, tile] = multiply(inverse_ref[mine, :], products)
 
     rows = pl.ds(pl.multiple_of(pl.program_id(0) * PANEL, PANEL), PANEL)
-    panel = jnp.concatenate([panel_ref[p, rows, :] for p in range(pieces)], axis=1)
-    basis = multiply(panel, inverse_ref[...], ((1,), (1,)))
+    basis = jnp.concatenate([panel_ref[p, rows, :] for p in range(pieces)], axis=1)
     high, low = split(basis)
     both = jnp.concatenate([high, low], axis=0)
     for t in range(0, cols, TILE):
@@ -388,8 +404,8 @@
             pltpu.VMEM((pieces, LANES, cols), jnp.float32),
             dma((blocks,)),
             dma((chunks,)),
-            dma((chunks,)),
-            dma((chunks,)),
+            dma((chunks * CHUNK // SENT,)),
+            dma((chunks * CHUNK // SENT,)),
             dma((levels,)),
             dma((levels,)),
             dma((col_n,)),

time: 109 us -> 114 us (1.046)
  Pallas kernels: 109 us -> 113 us
    pallas_call x1, Pallas kernels: 90.3 us -> 99.7 us  [shards(): pl.pallas_call(functools.partial(gather_kernel, row_n, col_n), out_shape=...]
    pallas_call x1, Pallas kernels: 18.3 us -> 13.3 us  [shards(): pl.pallas_call(functools.partial(project_kernel, rows * row_n, share_rows...]
where the time goes in v3:
time: 114 us
  Pallas kernels  113 us (99%)
    pallas_call x1, Pallas kernels, shards(): pl.pallas_call(functools.partial(gather_kernel, row_n, col_n), out_shape=...  99.7 us
    pallas_call x1, Pallas kernels, shards(): pl.pallas_call(functools.partial(project_kernel, rows * row_n, share_rows...  13.3 us

profile of v3, /device:TPU:27, one launch (start us, length us, event | category | flops | bytes accessed | tf_op | source)
XLA Modules:
  0.0 113.7 jit_solution(14845142402195248481)
XLA Ops:
  0.6 99.7 %gather.1 = (f32[2,2048,128]{2,1,0:T(8,128)S(1)}, f32[256,256]{1,0:T(8,128)S(1)}, f32[2,128,2048]{2,1,0:T(8,128)S(1)}, f32[2048,2048]{1,0:T(8,128)S(1)}) custom-call(f32[2048,2048]{1,0:T(8,128)} %matrix_ref.1), custom_call_target="tpu_custom_call" | custom-call | tf_op jit(solution)/shard_map/gather/pallas_call | solution.py:389
  100.3 13.3 %project.1 = (f32[32,2048]{1,0:T(8,128)}, f32[2048,2048]{1,0:T(8,128)}) custom-call(f32[2048,2048]{1,0:T(8,128)S(1)} %get-tuple-element.6.matrix_ref, f32[2,2048,128]{2,1,0:T(8,128)S(1)} %get-tuple-element.7.panel_ref, f32[256,256]{1,0:T(8,128)S(1)} %get-tuple-element.8.inverse_ref, f32[2,128,2048]{2,1,0:T(8,128)S(1)} %get-tuple-element.9.products_ref), custom_call_target="tpu_custom_call" | custom-call | tf_op jit(solution)/shard_map/project/pallas_call | solution.py:423
